TPU v7x, 32 devices: a whole 2x2x4 slice. The times are simulated.
32 devices in a mesh: front: 4 (over x, core), grid: 8 (over z, y).
Axes of the slice: x: 2, y: 2, z: 4, core: 2. Of those that a mesh axis runs over, the one named last changes fastest.
Arguments:
- index_map: int32 [4, 8192], P('front'), may hold values from 0 to 16383, as said below
- lengths: int32 [4], P('front'), may hold values from 1 to 8192, 24576 in all
- update_front: float32 [4, 8192, 8192], P('front', 'grid'), may hold values from -0.0625 to 0.0625
- front_matrix: float32 [16384, 16384], P(('front', 'grid')), may hold values from -0.046875 to 0.046875
- random: float32 [16384, 256], P(('front', 'grid')), may hold values from -6 to 6
Outputs:
- parent_sample: float32 [16384, 256], P(('front', 'grid'))
Inputs may be any that keep to these rules, and one draw needn't show every extreme that they name: `index_map`: within one child the 8192 entries are distinct parent rows. `lengths`: rows of a child at or past its length are not live; the largest length equals 8192.
All inputs are finite; a program needn't handle non-finite values. No bound on the sum of `lengths` on one device may be relied on, other than what follows from the above.
Results may differ from a plain program's by a relative error of at most 0.0003.
Values sent between devices are 32-bit elements; how exact they have to be, the bound alone decides.
A program may use at most 192 MiB of HBM per device.

v0:
```python
import jax
import jax.numpy as jnp
from jax import lax
from jax.sharding import PartitionSpec as P


def shards(index_map, lengths, update_front, front_matrix, random):
    gathered_random = lax.all_gather(random, ("front", "grid"), axis=0, tiled=True)
    parent_part = jnp.dot(
        front_matrix,
        gathered_random,
        preferred_element_type=jnp.float32,
        precision=lax.Precision.HIGHEST,
    )
    index_rows = index_map[0]
    child_random = jnp.take(gathered_random, index_rows, axis=0)
    child_sample = jnp.dot(
        update_front[0],
        child_random,
        preferred_element_type=jnp.float32,
        precision=lax.Precision.HIGHEST,
    )
    local_rows = child_sample.shape[0]
    first_row = lax.axis_index("grid") * local_rows
    row_numbers = first_row + jnp.arange(local_rows, dtype=jnp.int32)
    live_rows = row_numbers < lengths[0]
    child_sample = jnp.where(live_rows[:, None], child_sample, jnp.float32(0.0))
    own_rows = parent_part.shape[0]
    group_sample = lax.all_gather(child_sample, "grid", axis=0, tiled=True)
    group_count = lax.axis_size("front")
    grid_count = lax.axis_size("grid")
    grid_place = lax.axis_index("grid")
    block_ids = jnp.arange(group_count, dtype=jnp.int32)[:, None] * grid_count + grid_place
    targets = (block_ids * own_rows + jnp.arange(own_rows, dtype=jnp.int32)[None, :]).reshape(-1)
    one_hot = (targets[:, None] == index_rows[None, :]).astype(jnp.float32)
    terms = jnp.dot(
        one_hot, group_sample, preferred_element_type=jnp.float32, precision=lax.Precision.HIGHEST
    )
    terms = terms.reshape(group_count, own_rows, terms.shape[1])
    added = lax.psum_scatter(terms, "front", scatter_dimension=0, tiled=True)[0]
    return parent_part + added


def solution(mesh):
    placed = (
        P("front", None),
        P("front"),
        P("front", "grid", None),
        P(("front", "grid"), None),
        P(("front", "grid"), None),
    )
    return jax.shard_map(
        shards, mesh=mesh, in_specs=placed, out_specs=P(("front", "grid"), None), check_vma=False
    )
```

profile of v0, /device:TPU:0, one launch (start us, length us, event | category | flops | bytes accessed | tf_op | source)
XLA Modules:
  0.0 452.4 jit_solution(5761068284359675660)
XLA Ops:
  6.5 0.0 all-gather.3.cloned.1.call-start
  6.5 0.7 all-gather.3.cloned.1.call-update
  7.3 0.0 all-gather.5.cloned.1.call-start
  8.0 0.8 compare_and_fusion
  8.7 0.8 compare_select_fusion
  9.6 118.0 %all-gather.3.cloned.1.call-done = f32[16384,256]{1,0:T(8,128)} async-done(((f32[512,256]{1,0:T(8,128)}), f32[16384,256]{1,0:T(8,128)}) %all-gather.3.cloned.1.call-update) | async-done | bytes 16777232 | tf_op jit(solution)/shard_map/all_gather | solution.py:8
  127.5 37.1 %gather_fusion = f32[8192,256]{1,0:T(8,128)} fusion(f32[16384,256]{1,0:T(8,128)} %all-gather.3.cloned.1.call-done, s32[8192]{0:T(1024)S(1)} %broadcast_clamp_fusion), kind=kCustom, calls=%fused_computation | custom fusion | bytes 16809984 | tf_op jit(solution)/shard_map/jit(_take)/gather | solution.py:16
  164.7 0.0 copy-start
  164.7 59.7 %fusion.14 = f32[1024,256]{0,1:T(8,128)} fusion(f32[1,1024,8192]{2,1,0:T(8,128)} %param.7, f32[8192,256]{1,0:T(8,128)} %gather_fusion, pred[8192]{0:T(1024)(128)(4,1)S(1)} %compare_and_fusion, pred[1024]{0:T(1024)(128)(4,1)S(1)} %add_compare_fusion), kind=kOutput, calls=%fused_computation.11 | convolution fusion | flops 25772163072 | bytes 43000832 | tf_op jit(solution)/shard_map/dot_general | solution.py:17
  224.3 0.0 all-gather.5.cloned.1.call-update
  224.3 0.2 reduce-scatter.2.cloned.1.call-start
  224.6 0.1 add_bitcast_fusion
  224.7 122.5 %all-gather.5.cloned.1.call-done = f32[8192,256]{0,1:T(8,128)} async-done(((f32[1024,256]{0,1:T(8,128)}), f32[8192,256]{0,1:T(8,128)}) %all-gather.5.cloned.1.call-update) | async-done | bytes 8388624 | tf_op jit(solution)/shard_map/all_gather | solution.py:29
  347.2 0.0 copy-done
  347.2 36.9 %fusion = f32[2048,256]{1,0:T(8,128)} fusion(f32[8192,256]{0,1:T(8,128)} %all-gather.5.cloned.1.call-done, s32[8192]{0:T(1024)S(1)} %bitcast.26, s32[2048]{0:T(1024)S(1)} %bitcast.28), kind=kOutput, calls=%fused_computation.1 | convolution fusion | flops 51556384768 | bytes 10526720 | tf_op jit(solution)/shard_map/dot_general | solution.py:36
  384.1 0.0 reduce-scatter.2.cloned.1.call-update
  384.1 29.5 %reduce-scatter.2.cloned.1.call-done = f32[1,512,256]{2,1,0:T(8,128)} async-done(((f32[4,512,256]{2,1,0:T(8,128)}), f32[1,512,256]{2,1,0:T(8,128)}) %reduce-scatter.2.cloned.1.call-update) | async-done | bytes 524304 | tf_op jit(solution)/shard_map/reduce_scatter | solution.py:40
  413.6 32.3 %convolution_add_fusion = f32[512,256]{1,0:T(8,128)} fusion(f32[512,16384]{1,0:T(8,128)} %param.8, f32[16384,256]{1,0:T(8,128)} %all-gather.3.cloned.1.call-done, f32[1,512,256]{2,1,0:T(8,128)} %reduce-scatter.2.cloned.1.call-done), kind=kOutput, calls=%fused_computation.12 | convolution fusion | flops 25769934848 | bytes 51380224 | tf_op jit(solution)/shard_map/dot_general | solution.py:9
  (4 shorter events, 0.0 us)
Async XLA Ops:
  6.5 121.0 %all-gather.3.cloned.1.call-start = ((), (), s32[]{:S(2)}) async-start(), calls=%async_computation.1 | async-start | bytes 17301504 | tf_op jit(solution)/shard_map/all_gather | solution.py:8
  7.3 339.9 %all-gather.5.cloned.1.call-start = ((), (), s32[]{:S(2)}) async-start(), calls=%async_computation.2 | async-start | bytes 9437184 | tf_op jit(solution)/shard_map/all_gather | solution.py:29
  164.7 182.5 %copy-start = (s32[1,8192]{1,0:T(1,128)S(1)}, s32[1,8192]{1,0:T(1,128)}, u32[]{:S(2)}) copy-start(s32[1,8192]{1,0:T(1,128)} %param.5) | copy-start | bytes 98308
  224.3 189.2 %reduce-scatter.2.cloned.1.call-start = ((), (), s32[]{:S(2)}) async-start(), calls=%async_computation.3 | async-start | bytes 2621440 | tf_op jit(solution)/shard_map/reduce_scatter | solution.py:40
Sparse Core Ops, SparseCore 0:
  10.4 117.0 all-gather.2
  224.5 122.6 all-gather.4
  384.2 29.3 reduce-scatter.1
where the time goes:
time: 453 us; the launch traced here: 452 us
  waiting for transfers between devices  271 us (60%)
  matrix products  129 us (28%)
  local copies, waits for them, and re-layouts  37.2 us (8%)
  between operations  13.8 us (3%)
    all_gather x1, waiting for transfers between devices, shards(): group_sample = lax.all_gather(child_sample, 'grid', axis=0, tiled=True)  123 us
    all_gather x1, waiting for transfers between devices, shards(): lax.all_gather(random, ('front', 'grid'), axis=0, tiled=True)  118 us
    dot_general x1, matrix products, shards(): jnp.dot(update_front[0], child_random, preferred_element_type=jnp.float32...  59.7 us
    gather x1, local copies, waits for them, and re-layouts, shards(): child_random = jnp.take(gathered_random, index_rows, axis=0)  37.1 us
    dot_general x1, matrix products, shards(): jnp.dot(one_hot, group_sample, preferred_element_type=jnp.float32, precis...  36.9 us
    dot_general x1, matrix products, shards(): jnp.dot(front_matrix, gathered_random, preferred_element_type=jnp.float32...  32.3 us
    reduce_scatter x1, waiting for transfers between devices, shards(): added = lax.psum_scatter(terms, 'front', scatter_dimension=0, tiled=True)[0]  29.5 us
  transfers between devices with their start and end apart: 3, of which 3 were waited for; matrix products, arithmetic and copies ran while one was open for 0% of the time, Pallas kernels for 0%

commit v1 on v0

v1 whole, which is shorter than its diff:
```python
import jax
import jax.numpy as jnp
from jax import lax
from jax.sharding import PartitionSpec as P


def product(a, b):
    return jnp.dot(a, b, preferred_element_type=jnp.float32, precision=lax.Precision.HIGH)


def shards(index_map, lengths, update_front, front_matrix, random):
    gathered_random = lax.all_gather(random, ("front", "grid"), axis=0, tiled=True)
    own_rows = front_matrix.shape[0]
    half = own_rows // 2
    index_rows = index_map[0]
    child_random = jnp.take(gathered_random, index_rows, axis=0)
    child_sample = product(update_front[0], child_random)
    local_rows = child_sample.shape[0]
    first_row = lax.axis_index("grid") * local_rows
    row_numbers = first_row + jnp.arange(local_rows, dtype=jnp.int32)
    live_rows = row_numbers < lengths[0]
    child_sample = jnp.where(live_rows[:, None], child_sample, jnp.float32(0.0))
    child_sample, gathered_random = lax.optimization_barrier((child_sample, gathered_random))
    group_sample = lax.all_gather(child_sample, "grid", axis=0, tiled=True)
    upper = product(front_matrix[:half], gathered_random)
    group_sample, upper = lax.optimization_barrier((group_sample, upper))
    group_count = lax.axis_size("front")
    grid_count = lax.axis_size("grid")
    grid_place = lax.axis_index("grid")
    block_ids = jnp.arange(group_count, dtype=jnp.int32)[:, None] * grid_count + grid_place
    targets = (block_ids * own_rows + jnp.arange(own_rows, dtype=jnp.int32)[None, :]).reshape(-1)
    one_hot = (targets[:, None] == index_rows[None, :]).astype(jnp.bfloat16)
    coarse = lax.reduce_precision(group_sample, 8, 7)
    rest = group_sample - coarse
    halves = jnp.concatenate([coarse, rest], axis=1).astype(jnp.bfloat16)
    both = jnp.dot(one_hot, halves, preferred_element_type=jnp.float32)
    width = group_sample.shape[1]
    terms = both[:, :width] + both[:, width:]
    terms = terms.reshape(group_count, own_rows, width)
    terms, gathered_random = lax.optimization_barrier((terms, gathered_random))
    added = lax.psum_scatter(terms, "front", scatter_dimension=0, tiled=True)[0]
    lower = product(front_matrix[half:], gathered_random)
    added, lower = lax.optimization_barrier((added, lower))
    return jnp.concatenate([upper, lower], axis=0) + added


def solution(mesh):
    placed = (
        P("front", None),
        P("front"),
        P("front", "grid", None),
        P(("front", "grid"), None),
        P(("front", "grid"), None),
    )
    return jax.shard_map(
        shards, mesh=mesh, in_specs=placed, out_specs=P(("front", "grid"), None), check_vma=False
    )
```

time: 453 us -> 392 us (0.87)
  waiting for transfers between devices: 271 us -> 226 us
  matrix products: 129 us -> 100 us
  other arithmetic: 1.66 us -> 11.2 us
    dot_general x3 -> x4, matrix products: 129 us -> 100 us  [the longest x3 78.4 us: product(): jnp.dot(a, b, preferred_element_type=jnp.float32, precision=lax.Precision...]
    reduce_scatter x1, waiting for transfers between devices: 29.5 us -> 6.93 us  [shards(): added = lax.psum_scatter(terms, 'front', scatter_dimension=0, tiled=True)[0]]
    all_gather x1, waiting for transfers between devices: 123 us -> 99.9 us  [shards(): group_sample = lax.all_gather(child_sample, 'grid', axis=0, tiled=True)]
    another operation x0 -> x1, other arithmetic: none -> 8.15 us
  transfers between devices with their start and end apart: 3 -> 3, of which waited for: 3 -> 3; matrix products, arithmetic and copies ran while one was open for 0% -> 12% of each run, Pallas kernels for 0% -> 0%
where the time goes in v1:
time: 392 us; the launch traced here: 391 us
  waiting for transfers between devices  226 us (58%)
  matrix products  100 us (26%)
  local copies, waits for them, and re-layouts  40.2 us (10%)
  between operations  13.8 us (4%)
  other arithmetic  11.2 us (3%)
    all_gather x1, waiting for transfers between devices, shards(): lax.all_gather(random, ('front', 'grid'), axis=0, tiled=True)  118 us
    all_gather x1, waiting for transfers between devices, shards(): group_sample = lax.all_gather(child_sample, 'grid', axis=0, tiled=True)  99.9 us
    dot_general x3, matrix products, product(): jnp.dot(a, b, preferred_element_type=jnp.float32, precision=lax.Precision...  78.4 us
    gather x1, local copies, waits for them, and re-layouts, shards(): child_random = jnp.take(gathered_random, index_rows, axis=0)  37.3 us
    dot_general x1, matrix products, shards(): both = jnp.dot(one_hot, halves, preferred_element_type=jnp.float32)  21.8 us
    another operation x1, other arithmetic  8.15 us
  transfers between devices with their start and end apart: 3, of which 3 were waited for; matrix products, arithmetic and copies ran while one was open for 12% of the time, Pallas kernels for 0%

profile of v1, /device:TPU:0, one launch (start us, length us, event | category | flops | bytes accessed | tf_op | source)
XLA Modules:
  0.0 391.2 jit_solution(2507641239275346115)
XLA Ops:
  6.5 0.0 all-gather.3.cloned.1.call-start
  6.5 0.7 all-gather.3.cloned.1.call-update
  7.3 0.0 all-gather.5.cloned.1.call-start
  8.0 0.8 compare_and_fusion
  8.7 0.8 compare_select_fusion
  9.6 118.0 %all-gather.3.cloned.1.call-done = f32[16384,256]{1,0:T(8,128)} async-done(((f32[512,256]{1,0:T(8,128)}), f32[16384,256]{1,0:T(8,128)}) %all-gather.3.cloned.1.call-update) | async-done | bytes 16777232 | tf_op jit(solution)/shard_map/all_gather | solution.py:12
  127.5 37.3 %gather_fusion = f32[8192,256]{1,0:T(8,128)} fusion(f32[16384,256]{1,0:T(8,128)} %all-gather.3.cloned.1.call-done, s32[8192]{0:T(1024)S(1)} %broadcast_clamp_fusion), kind=kCustom, calls=%fused_computation | custom fusion | bytes 16809984 | tf_op jit(solution)/shard_map/jit(_take)/gather | solution.py:16
  164.8 33.2 %fusion.22 = f32[1024,256]{0,1:T(8,128)} fusion(f32[1,1024,8192]{2,1,0:T(8,128)} %param.7, f32[8192,256]{1,0:T(8,128)} %gather_fusion, pred[8192]{0:T(1024)(128)(4,1)S(1)} %compare_and_fusion, pred[1024]{0:T(1024)(128)(4,1)S(1)} %add_compare_fusion), kind=kOutput, calls=%fused_computation.22 | convolution fusion | flops 12887261184 | bytes 43000832 | tf_op jit(solution)/shard_map/dot_general | solution.py:8
  198.0 0.0 all-gather.5.cloned.1.call-update
  198.1 0.2 reduce-scatter.2.cloned.1.call-start
  198.3 0.1 add_bitcast_fusion
  198.4 22.6 %fusion.27 = f32[256,256]{0,1:T(8,128)S(1)} fusion(f32[16384,256]{1,0:T(8,128)} %all-gather.3.cloned.1.call-done, f32[512,16384]{1,0:T(8,128)} %param.8), kind=kOutput, calls=%fused_computation.23 | convolution fusion | flops 6442450944 | bytes 33816576 | tf_op jit(solution)/shard_map/dot_general | solution.py:8
  221.0 0.0 copy-start
  221.0 99.9 %all-gather.5.cloned.1.call-done = f32[8192,256]{0,1:T(8,128)} async-done(((f32[1024,256]{0,1:T(8,128)}), f32[8192,256]{0,1:T(8,128)}) %all-gather.5.cloned.1.call-update) | async-done | bytes 8388624 | tf_op jit(solution)/shard_map/all_gather | solution.py:24
  320.9 8.1 %reduce-precision_convert_fusion = (bf16[8192,256]{0,1:T(8,128)(2,1)}, bf16[8192,256]{0,1:T(8,128)(2,1)}) fusion(f32[8192,256]{0,1:T(8,128)} %all-gather.5.cloned.1.call-done), kind=kLoop, calls=%fused_computation.12 | loop fusion | flops 8388608 | bytes 16777216 | tf_op jit(solution)/shard_map/convert
  329.1 0.0 copy-done
  329.1 21.8 %fusion = f32[2048,512]{1,0:T(8,128)S(1)} fusion(s32[8192]{0:T(1024)S(1)} %bitcast.29, s32[2048]{0:T(1024)S(1)} %bitcast.31, bf16[8192,256]{0,1:T(8,128)(2,1)} %get-tuple-element.22, bf16[8192,256]{0,1:T(8,128)(2,1)} %get-tuple-element.21), kind=kOutput, calls=%fused_computation.1 | convolution fusion | flops 17213423616 | bytes 12623872 | tf_op jit(solution)/shard_map/dot_general | solution.py:36
  350.9 0.3 slice_add_fusion
  351.2 1.9 copy.7
  353.1 0.0 reduce-scatter.2.cloned.1.call-update
  353.1 22.6 %fusion.30 = f32[256,256]{0,1:T(8,128)S(1)} fusion(f32[16384,256]{1,0:T(8,128)} %all-gather.3.cloned.1.call-done, f32[512,16384]{1,0:T(8,128)} %param.8), kind=kOutput, calls=%fused_computation.24 | convolution fusion | flops 6442450944 | bytes 33816576 | tf_op jit(solution)/shard_map/dot_general | solution.py:8
  375.7 6.9 %reduce-scatter.2.cloned.1.call-done = f32[1,512,256]{1,2,0:T(8,128)} async-done(((f32[4,512,256]{1,2,0:T(8,128)}), f32[1,512,256]{1,2,0:T(8,128)}) %reduce-scatter.2.cloned.1.call-update) | async-done | bytes 524304 | tf_op jit(solution)/shard_map/reduce_scatter | solution.py:41
  382.6 1.1 maximum_add_fusion
  383.7 1.0 copy.8
  (4 shorter events, 0.0 us)
Async XLA Ops:
  6.5 121.0 %all-gather.3.cloned.1.call-start = ((), (), s32[]{:S(2)}) async-start(), calls=%async_computation.1 | async-start | bytes 17301504 | tf_op jit(solution)/shard_map/all_gather | solution.py:12
  7.3 313.7 %all-gather.5.cloned.1.call-start = ((), (), s32[]{:S(2)}) async-start(), calls=%async_computation.2 | async-start | bytes 9437184 | tf_op jit(solution)/shard_map/all_gather | solution.py:24
  198.1 184.5 %reduce-scatter.2.cloned.1.call-start = ((), (), s32[]{:S(2)}) async-start(), calls=%async_computation.3 | async-start | bytes 2621440 | tf_op jit(solution)/shard_map/reduce_scatter | solution.py:41
  221.0 108.1 %copy-start = (s32[1,8192]{1,0:T(1,128)S(1)}, s32[1,8192]{1,0:T(1,128)}, u32[]{:S(2)}) copy-start(s32[1,8192]{1,0:T(1,128)} %param.5) | copy-start | bytes 98308
Sparse Core Ops, SparseCore 0:
  10.4 117.0 all-gather.2
  198.2 122.6 all-gather.4
  353.2 29.3 reduce-scatter.1
